TPU v7x, 32 devices: a whole 2x2x4 slice. The times are simulated.
32 devices in a mesh: rep: 8 (over y, x, core), shard: 4 (over z).
Axes of the slice: x: 2, y: 2, z: 4, core: 2. Of those that a mesh axis runs over, the one named last changes fastest.
Arguments:
- activations: bfloat16 [6, 4096, 2048], P(None, ('rep', 'shard')), may hold values from -50 to 50
- cotangents: bfloat16 [6, 4096, 512], P(None, ('rep', 'shard')), may hold values from -120 to 120
- momentum: float32 [12, 256, 2048], P(None, None, 'shard'), may hold values from -6 to 6
- owners: int32 [12], replicated, may hold values from 0 to 3, as said below
- bucket_starts: int32 [2], replicated, may hold values from 1 to 11, as said below
Outputs:
- momentum_out: float32 [12, 256, 2048], P(None, None, 'shard')
- update: float32 [12, 256, 2048], P(None, None, 'shard')
- owned: bfloat16 [16, 256, 2048], P('shard')
Inputs may be any that keep to these rules, and one draw needn't show every extreme that they name: `owners`: no owner is named more than 4 times, and some owner exactly 4 times. `bucket_starts`: strictly increasing.
All inputs are finite; a program needn't handle non-finite values.
Results may differ from a plain program's by a relative error of at most 0.033.
Values may be sent and summed in bfloat16 or wider, within the bound.
No kernel may reach another device: no remote copies, remote signals or barrier semaphores. Data moves between devices by JAX's collectives and lax.ppermute only.
A program may use at most 128 MiB of HBM per device.

v0:
```python
import math
import jax
import jax.numpy as jnp
from jax import lax
from jax.sharding import PartitionSpec as P

D = 2048
KV = 256
ITERS = 5
MATS = 12
coef_a = 3.4445
coef_b = -4.775
coef_c = 2.0315
momentum_rate = 0.95
clip_level = 0.5
epsilon = 1e-06


def orthogonal_batch(matrices):
    values = matrices.astype(jnp.float32)
    frobenius = jnp.sqrt(jnp.sum(values * values, axis=(1, 2), keepdims=True))
    matrix = (values / (frobenius + epsilon)).astype(jnp.bfloat16)
    for iteration in range(ITERS):
        gram_matrix = jnp.einsum(
            "skd,sjd->skj", matrix, matrix, preferred_element_type=jnp.float32
        ).astype(jnp.bfloat16)
        square = jnp.einsum(
            "skj,sji->ski", gram_matrix, gram_matrix, preferred_element_type=jnp.float32
        )
        mixing = (coef_b * gram_matrix.astype(jnp.float32) + coef_c * square).astype(jnp.bfloat16)
        product = jnp.einsum("skj,sjd->skd", mixing, matrix, preferred_element_type=jnp.float32)
        matrix = (coef_a * matrix.astype(jnp.float32) + product).astype(jnp.bfloat16)
    return matrix


def clip_factors(square_sums, bucket_starts):
    indices = jnp.arange(MATS, dtype=jnp.int32)
    buckets = jnp.sum((indices[:, None] >= bucket_starts[None, :]).astype(jnp.int32), axis=1)
    together = (buckets[:, None] == buckets[None, :]).astype(jnp.float32)
    totals = jnp.sum(together * square_sums[None, :], axis=1)
    members = jnp.sum(together, axis=1)
    root_mean = jnp.sqrt(totals / (members * KV * D) + epsilon)
    return jnp.minimum(1.0, clip_level / root_mean)


def slot_numbers(owners):
    indices = jnp.arange(MATS, dtype=jnp.int32)
    earlier = (indices[None, :] < indices[:, None]) & (owners[None, :] == owners[:, None])
    return jnp.sum(earlier.astype(jnp.int32), axis=1)


def selector(owner_of, slot_of, shard_count, slot_count):
    holders = lax.broadcasted_iota(jnp.int32, (shard_count, slot_count, 1), 0)
    places = lax.broadcasted_iota(jnp.int32, (shard_count, slot_count, 1), 1)
    chosen = (holders == owner_of[None, None, :]) & (places == slot_of[None, None, :])
    return chosen.astype(jnp.bfloat16)


def pack_slots(shards, chooser):
    return jnp.einsum("psm,mkd->skpd", chooser, shards, preferred_element_type=jnp.float32).astype(
        jnp.bfloat16
    )


def unpack_slots(received, chooser):
    return jnp.einsum("psm,skpd->mkd", chooser, received, preferred_element_type=jnp.float32)


def per_device(activations, cotangents, momentum, owners, bucket_starts):
    shard_count = lax.axis_size("shard")
    replica_count = lax.axis_size("rep")
    layers, tok_rows, width = activations.shape
    token_total = tok_rows * shard_count * replica_count
    columns = width // shard_count
    slot_count = -(-MATS // shard_count) + 1
    update_scale = math.sqrt(max(KV, D))
    partial_terms = jnp.einsum(
        "ltk,ltd->lkd", cotangents, activations, preferred_element_type=jnp.float32
    ).reshape(MATS, KV, width)
    shard_part = lax.psum_scatter(
        partial_terms.astype(jnp.bfloat16), "shard", scatter_dimension=2, tiled=True
    )
    summed = lax.psum(shard_part, "rep").astype(jnp.float32)
    gradient = summed / jnp.sqrt(jnp.float32(token_total))
    square_sums = lax.psum(jnp.sum(gradient * gradient, axis=(1, 2)), "shard")
    factors = clip_factors(square_sums, bucket_starts)
    momentum_out = momentum_rate * momentum + factors[:, None, None] * gradient
    nesterov = (factors[:, None, None] * gradient + momentum_rate * momentum_out).astype(
        jnp.bfloat16
    )
    slot_of = slot_numbers(owners)
    chooser = selector(owners, slot_of, shard_count, slot_count)
    received = lax.all_to_all(
        pack_slots(nesterov, chooser), "shard", split_axis=2, concat_axis=2, tiled=True
    )
    item_count = received.shape[0]
    result = orthogonal_batch(received.reshape(item_count, KV, width))
    scaled = (update_scale * result.astype(jnp.float32)).astype(jnp.bfloat16)
    returned_part = lax.all_to_all(
        result.reshape(item_count, KV, shard_count, columns),
        "shard",
        split_axis=2,
        concat_axis=2,
        tiled=True,
    )
    update = update_scale * unpack_slots(returned_part, chooser)
    return (momentum_out, update, scaled)


def solution(mesh):
    placed = (
        P(None, ("rep", "shard"), None),
        P(None, ("rep", "shard"), None),
        P(None, None, "shard"),
        P(),
        P(),
    )
    return jax.shard_map(
        per_device,
        mesh=mesh,
        in_specs=placed,
        out_specs=(P(None, None, "shard"), P(None, None, "shard"), P("shard", None, None)),
        check_vma=False,
    )
```

profile of v0, /device:TPU:0, one launch (start us, length us, event | category | flops | bytes accessed | tf_op | source)
XLA Modules:
  0.0 628.7 jit_solution(7850183555704222649)
XLA Ops:
  7.2 1.8 copy-done
  9.1 7.5 %convolution_convert_fusion = bf16[6,512,2048]{2,1,0:T(8,128)(2,1)} fusion(bf16[6,128,512]{2,1,0:T(8,128)(2,1)} %param.6, bf16[6,128,2048]{2,1,0:T(8,128)(2,1)S(1)} %copy-done), kind=kOutput, calls=%fused_computation.13 | convolution fusion | flops 1616904192 | bytes 16515072 | tf_op jit(solution)/shard_map/ltk,ltd->lkd/dot_general | solution.py:77
  16.7 214.7 %reduce-scatter.2.cloned.1.call-done = bf16[12,256,512]{2,1,0:T(8,128)(2,1)} async-done(((bf16[12,256,2048]{2,1,0:T(8,128)(2,1)}), bf16[12,256,512]{2,1,0:T(8,128)(2,1)}) %reduce-scatter.2.cloned.1.call-update) | async-done | bytes 3145744 | tf_op jit(solution)/shard_map/reduce_scatter | solution.py:80
  231.4 0.2 convert_reduce_fusion
  231.6 73.4 %all-reduce.2.cloned.1.call-done = bf16[12,256,512]{2,1,0:T(8,128)(2,1)} async-done(((bf16[12,256,512]{2,1,0:T(8,128)(2,1)}), bf16[12,256,512]{2,1,0:T(8,128)(2,1)}) %all-reduce.2.cloned.1.call-update) | async-done | bytes 3145744 | tf_op jit(solution)/shard_map/psum | solution.py:83
  305.0 2.9 fusion.4
  308.0 11.7 %psum.15 = f32[12]{0:T(128)S(1)} all-reduce(f32[12]{0:T(128)S(1)} %fusion.4), channel_id=1, replica_groups=mesh['rep'=8,'shard'=4] {'shard'}, use_global_device_ids=true, to_apply=%region_4.0 | all-reduce | flops 12 | bytes 96 | tf_op jit(solution)/shard_map/psum | solution.py:85
  319.7 0.2 fusion.41
  319.9 8.1 %fusion.9 = (bf16[12,256,512,1]{2,1,0,3:T(8,128)(2,1)S(1)}, f32[12,256,512]{2,1,0:T(8,128)}) fusion(bf16[12,256,512]{2,1,0:T(8,128)(2,1)} %all-reduce.2.cloned.1.call-done, f32[12]{0:T(128)S(1)} %minimum_multiply_fusion, f32[12,256,512]{2,1,0:T(8,128)} %param.7), kind=kLoop, calls=%fused_computation.20 | loop fusion | flops 11010048 | bytes 18874416 | tf_op jit(solution)/shard_map/convert_element_type | solution.py:88
  327.9 2.8 fusion.6
  330.7 1.4 copy.28
  332.2 94.6 %all_to_all.10 = bf16[4,256,4,512]{3,0,1,2:T(4,128)(2,1)} all-to-all(bf16[4,256,4,512]{3,0,1,2:T(4,128)(2,1)S(1)} %copy.28), channel_id=1, replica_groups=mesh['rep'=8,'shard'=4] {'shard'}, dimensions={2} | all-to-all | bytes 8388608 | tf_op jit(solution)/shard_map/all_to_all | solution.py:93
  426.8 7.5 %copy.29 = bf16[4,256,4,512]{1,3,2,0:T(8,128)(2,1)} copy(bf16[4,256,4,512]{3,0,1,2:T(4,128)(2,1)} %all_to_all.10) | data formatting | bytes 8388608 | tf_op jit(solution)/shard_map/all_to_all | solution.py:93
  434.3 3.4 multiply_reduce_fusion
  437.6 6.9 %copy.30 = f32[4,256,2048]{2,1,0:T(8,128)} copy(bf16[4,256,2048]{1,2,0:T(8,128)(2,1)} %bitcast.48) | data formatting | bytes 12582912 | tf_op jit(solution)/shard_map/convert_element_type | solution.py:20
  444.6 4.6 divide_convert_fusion
  449.2 2.0 copy-done.2
  451.2 1.3 convolution_convert_fusion.6
  452.5 6.3 add_convert_fusion.4
  458.7 4.7 convolution_convert_fusion.5
  463.5 6.3 add_convert_fusion.3
  469.7 4.8 convolution_convert_fusion.4
  474.5 6.3 add_convert_fusion.2
  480.8 4.7 convolution_convert_fusion.3
  485.5 6.3 add_convert_fusion.1
  491.8 4.7 convolution_convert_fusion.2
  496.6 7.7 %multiply_convert_fusion = (bf16[4,256,2048]{2,1,0:T(8,128)(2,1)}, bf16[4,256,2048]{2,1,0:T(8,128)(2,1)}) fusion(bf16[4,256,2048]{2,1,0:T(8,128)(2,1)} %add_convert_fusion.1, bf16[4,256,256]{2,1,0:T(8,128)(2,1)S(1)} %convolution_convert_fusion.2), kind=kOutput, calls=%fused_computation.1 | convolution fusion | flops 1223950336 | bytes 13107200 | tf_op jit(solution)/shard_map/skj,sjd->skd/dot_general | solution.py:31
  504.3 7.8 %reshape.38 = bf16[4,256,4,512]{3,2,1,0:T(4,128)(2,1)} reshape(bf16[4,256,2048]{2,1,0:T(8,128)(2,1)} %get-tuple-element.20) | data formatting | bytes 8388608 | tf_op jit(solution)/shard_map/reshape | solution.py:100
  512.1 5.4 copy.31
  517.5 94.6 %all_to_all.11 = bf16[4,256,4,512]{3,0,1,2:T(4,128)(2,1)S(1)} all-to-all(bf16[4,256,4,512]{3,0,1,2:T(4,128)(2,1)S(1)} %copy.31), channel_id=1, replica_groups=mesh['rep'=8,'shard'=4] {'shard'}, dimensions={2} | all-to-all | bytes 8388608 | tf_op jit(solution)/shard_map/all_to_all | solution.py:99
  612.2 3.4 bitcast_multiply_fusion
  615.5 6.3 %copy.33 = f32[12,256,512]{2,1,0:T(8,128)} copy(f32[12,256,512]{2,0,1:T(8,128)S(1)} %bitcast_multiply_fusion) | data formatting | bytes 12582912
  (15 shorter events, 0.2 us)
Async XLA Ops:
  7.2 1.9 copy-start
  7.2 224.2 %reduce-scatter.2.cloned.1.call-start = ((), (), s32[]{:S(2)}) async-start(), calls=%async_computation.3 | async-start | bytes 15728640 | tf_op jit(solution)/shard_map/reduce_scatter | solution.py:80
  16.6 214.8 %copy-start.3 = (s32[12]{0:T(128)S(1)}, s32[12]{0:T(128)}, u32[]{:S(2)}) copy-start(s32[12]{0:T(128)} %param.8) | copy-start | bytes 148
  16.6 291.3 %copy-start.4 = (s32[2]{0:T(128)S(1)}, s32[2]{0:T(128)}, u32[]{:S(2)}) copy-start(s32[2]{0:T(128)} %param.9) | copy-start | bytes 28
  16.6 288.4 %all-reduce.2.cloned.1.call-start = ((), (), s32[]{:S(2)}) async-start(), calls=%async_computation.4 | async-start | bytes 6291456 | tf_op jit(solution)/shard_map/psum | solution.py:83
  449.2 2.0 copy-start.2
  612.2 9.7 %copy-start.1 = (bf16[6,128,2048]{2,1,0:T(8,128)(2,1)S(1)}, bf16[6,128,2048]{2,1,0:T(8,128)(2,1)}, u32[]{:S(2)}) copy-start(bf16[6,128,2048]{2,1,0:T(8,128)(2,1)} %param.5) | copy-start | bytes 9437188
Sparse Core Ops, SparseCore 0:
  16.7 214.6 reduce-scatter.1
  234.7 70.3 all-reduce.1
where the time goes:
time: 630 us; the launch traced here: 629 us
  waiting for transfers between devices  288 us (46%)
  blocking collectives  201 us (32%)
  matrix products  66.7 us (11%)
  local copies, waits for them, and re-layouts  39.3 us (6%)
  other arithmetic  19.4 us (3%)
  between operations  14.1 us (2%)
    reduce_scatter x1, waiting for transfers between devices, per_device(): lax.psum_scatter(partial_terms.astype(jnp.bfloat16), 'shard', scatter_dim...  215 us
    all_to_all x1, blocking collectives, per_device(): lax.all_to_all(result.reshape(item_count, KV, shard_count, columns), 'sha...  94.6 us
    all_to_all x1, blocking collectives, per_device(): lax.all_to_all(pack_slots(nesterov, chooser), 'shard', split_axis=2, conc...  94.6 us
    psum x1, waiting for transfers between devices, per_device(): summed = lax.psum(shard_part, 'rep').astype(jnp.float32)  73.4 us
    dot_general x5, matrix products, orthogonal_batch(): jnp.einsum('skj,sjd->skd', mixing, matrix, preferred_element_type=jnp.flo...  32.7 us
    dot_general x5, matrix products, orthogonal_batch(): jnp.einsum('skd,sjd->skj', matrix, matrix, preferred_element_type=jnp.flo...  20.3 us
    reshape x2, local copies, waits for them, and re-layouts, per_device(): result.reshape(item_count, KV, shard_count, columns)  13.2 us
  transfers between devices with their start and end apart: 2, of which 2 were waited for; matrix products, arithmetic and copies ran while one was open for 0% of the time, Pallas kernels for 0%

commit v1 on v0

--- a/solution.py
+++ b/solution.py
@@ -90,9 +90,11 @@
     )
     slot_of = slot_numbers(owners)
     chooser = selector(owners, slot_of, shard_count, slot_count)
-    received = lax.all_to_all(
-        pack_slots(nesterov, chooser), "shard", split_axis=2, concat_axis=2, tiled=True
-    )
+    x = pack_slots(nesterov, chooser)
+    devices = lax.axis_size("shard")
+    tiles = jnp.stack(jnp.split(x, devices, axis=2), axis=0)
+    tiles = lax.all_to_all(tiles, "shard", split_axis=0, concat_axis=0)
+    received = jnp.concatenate(tiles, axis=2)
     item_count = received.shape[0]
     result = orthogonal_batch(received.reshape(item_count, KV, width))
     scaled = (update_scale * result.astype(jnp.float32)).astype(jnp.bfloat16)

time: 630 us -> 651 us (1.033)
  other arithmetic: 19.4 us -> 28.8 us
    convert_element_type x1 -> x2, local copies, waits for them, and re-layouts: 6.94 us -> 18.6 us  [orthogonal_batch(): values = matrices.astype(jnp.float32)]
    all_to_all x1 -> x0, local copies, waits for them, and re-layouts: 7.45 us -> none  [per_device(): lax.all_to_all(pack_slots(nesterov, chooser), 'shard', split_axis=2, conc...]
where the time goes in v1:
time: 651 us; the launch traced here: 643 us
  waiting for transfers between devices  288 us (44%)
  blocking collectives  201 us (31%)
  matrix products  66.9 us (10%)
  local copies, waits for them, and re-layouts  44.2 us (7%)
  other arithmetic  28.8 us (4%)
  between operations  14.4 us (2%)
    reduce_scatter x1, waiting for transfers between devices, per_device(): lax.psum_scatter(partial_terms.astype(jnp.bfloat16), 'shard', scatter_dim...  215 us
    all_to_all x1, blocking collectives, per_device(): lax.all_to_all(result.reshape(item_count, KV, shard_count, columns), 'sha...  94.9 us
    all_to_all x1, blocking collectives, per_device(): tiles = lax.all_to_all(tiles, 'shard', split_axis=0, concat_axis=0)  94.2 us
    psum x1, waiting for transfers between devices, per_device(): summed = lax.psum(shard_part, 'rep').astype(jnp.float32)  73.4 us
    dot_general x5, matrix products, orthogonal_batch(): jnp.einsum('skj,sjd->skd', mixing, matrix, preferred_element_type=jnp.flo...  32.9 us
    dot_general x5, matrix products, orthogonal_batch(): jnp.einsum('skd,sjd->skj', matrix, matrix, preferred_element_type=jnp.flo...  20.3 us
    convert_element_type x2, local copies, waits for them, and re-layouts, orthogonal_batch(): values = matrices.astype(jnp.float32)  18.6 us
    reshape x2, local copies, waits for them, and re-layouts, per_device(): result.reshape(item_count, KV, shard_count, columns)  13.2 us
  transfers between devices with their start and end apart: 2, of which 2 were waited for; matrix products, arithmetic and copies ran while one was open for 0% of the time, Pallas kernels for 0%

profile of v1, /device:TPU:0, one launch (start us, length us, event | category | flops | bytes accessed | tf_op | source)
XLA Modules:
  0.0 643.3 jit_solution(724655441479620508)
XLA Ops:
  7.2 1.8 copy-done
  9.1 7.5 %convolution_convert_fusion = bf16[6,512,2048]{2,1,0:T(8,128)(2,1)} fusion(bf16[6,128,512]{2,1,0:T(8,128)(2,1)} %param.6, bf16[6,128,2048]{2,1,0:T(8,128)(2,1)S(1)} %copy-done), kind=kOutput, calls=%fused_computation.15 | convolution fusion | flops 1616904192 | bytes 16515072 | tf_op jit(solution)/shard_map/ltk,ltd->lkd/dot_general | solution.py:77
  16.7 214.7 %reduce-scatter.2.cloned.1.call-done = bf16[12,256,512]{2,1,0:T(8,128)(2,1)} async-done(((bf16[12,256,2048]{2,1,0:T(8,128)(2,1)}), bf16[12,256,512]{2,1,0:T(8,128)(2,1)}) %reduce-scatter.2.cloned.1.call-update) | async-done | bytes 3145744 | tf_op jit(solution)/shard_map/reduce_scatter | solution.py:80
  231.6 73.4 %all-reduce.2.cloned.1.call-done = bf16[12,256,512]{2,1,0:T(8,128)(2,1)} async-done(((bf16[12,256,512]{2,1,0:T(8,128)(2,1)}), bf16[12,256,512]{2,1,0:T(8,128)(2,1)}) %all-reduce.2.cloned.1.call-update) | async-done | bytes 3145744 | tf_op jit(solution)/shard_map/psum | solution.py:83
  305.0 2.9 fusion.5
  308.0 11.7 %psum.15 = f32[12]{0:T(128)S(1)} all-reduce(f32[12]{0:T(128)S(1)} %fusion.5), channel_id=1, replica_groups=mesh['rep'=8,'shard'=4] {'shard'}, use_global_device_ids=true, to_apply=%region_4.0 | all-reduce | flops 12 | bytes 96 | tf_op jit(solution)/shard_map/psum | solution.py:85
  319.9 8.1 %fusion.10 = (bf16[12,256,512,1]{2,1,0,3:T(8,128)(2,1)S(1)}, f32[12,256,512]{2,1,0:T(8,128)}) fusion(bf16[12,256,512]{2,1,0:T(8,128)(2,1)} %all-reduce.2.cloned.1.call-done, f32[12]{0:T(128)S(1)} %minimum_multiply_fusion, f32[12,256,512]{2,1,0:T(8,128)} %param.7), kind=kLoop, calls=%fused_computation.23 | loop fusion | flops 11010048 | bytes 18874416 | tf_op jit(solution)/shard_map/convert_element_type | solution.py:88
  327.9 2.8 fusion.7
  330.7 2.2 slice_bitcast_fusion.3
  332.9 3.9 pad_maximum_fusion
  336.8 94.2 %all_to_all.10 = bf16[4,4,256,1,512]{4,1,2,3,0:T(4,128)(2,1)S(1)} all-to-all(bf16[4,4,256,1,512]{4,1,2,3,0:T(4,128)(2,1)S(1)} %pad_maximum_fusion), channel_id=1, replica_groups=mesh['rep'=8,'shard'=4] {'shard'}, dimensions={0} | all-to-all | bytes 8388608 | tf_op jit(solution)/shard_map/all_to_all | solution.py:96
  431.0 4.4 fusion
  435.4 4.5 convert_bitcast_fusion
  440.0 9.9 %copy.39 = f32[4,256,4,1,512]{1,4,2,0,3:T(8,128)} copy(f32[4,256,4,1,512]{4,0,1,3,2:T(4,128)} %convert_bitcast_fusion) | data formatting | bytes 16777216 | tf_op jit(solution)/shard_map/convert_element_type | solution.py:20
  449.9 8.7 %copy.40 = f32[4,256,2048]{2,1,0:T(8,128)} copy(f32[4,256,2048]{1,2,0:T(8,128)} %bitcast.63) | data formatting | bytes 16777216 | tf_op jit(solution)/shard_map/convert_element_type | solution.py:20
  458.6 4.6 divide_convert_fusion
  463.2 2.0 copy-done.2
  465.2 1.3 convolution_convert_fusion.6
  466.5 6.3 add_convert_fusion.4
  472.7 4.7 convolution_convert_fusion.5
  477.5 6.4 add_convert_fusion.3
  483.9 4.8 convolution_convert_fusion.4
  488.7 6.3 add_convert_fusion.2
  495.0 4.7 convolution_convert_fusion.3
  499.7 6.3 add_convert_fusion.1
  506.0 4.7 convolution_convert_fusion.2
  510.7 7.7 %multiply_convert_fusion = (bf16[4,256,2048]{2,1,0:T(8,128)(2,1)}, bf16[4,256,2048]{2,1,0:T(8,128)(2,1)}) fusion(bf16[4,256,2048]{2,1,0:T(8,128)(2,1)} %add_convert_fusion.1, bf16[4,256,256]{2,1,0:T(8,128)(2,1)S(1)} %convolution_convert_fusion.2), kind=kOutput, calls=%fused_computation.4 | convolution fusion | flops 1223950336 | bytes 13107200 | tf_op jit(solution)/shard_map/skj,sjd->skd/dot_general | solution.py:31
  518.4 7.8 %reshape.38 = bf16[4,256,4,512]{3,2,1,0:T(4,128)(2,1)} reshape(bf16[4,256,2048]{2,1,0:T(8,128)(2,1)} %get-tuple-element.24) | data formatting | bytes 8388608 | tf_op jit(solution)/shard_map/reshape | solution.py:102
  526.2 5.4 copy.41
  531.7 94.9 %all_to_all.11 = bf16[4,256,4,512]{3,0,1,2:T(4,128)(2,1)S(1)} all-to-all(bf16[4,256,4,512]{3,0,1,2:T(4,128)(2,1)S(1)} %copy.41), channel_id=1, replica_groups=mesh['rep'=8,'shard'=4] {'shard'}, dimensions={2} | all-to-all | bytes 8388608 | tf_op jit(solution)/shard_map/all_to_all | solution.py:101
  626.5 3.4 bitcast_multiply_fusion
  629.9 6.3 copy.43
  (17 shorter events, 0.6 us)
Async XLA Ops:
  7.2 1.9 copy-start
  7.2 224.2 %reduce-scatter.2.cloned.1.call-start = ((), (), s32[]{:S(2)}) async-start(), calls=%async_computation.3 | async-start | bytes 15728640 | tf_op jit(solution)/shard_map/reduce_scatter | solution.py:80
  16.6 214.8 %copy-start.3 = (s32[12]{0:T(128)S(1)}, s32[12]{0:T(128)}, u32[]{:S(2)}) copy-start(s32[12]{0:T(128)} %param.8) | copy-start | bytes 148
  16.6 291.3 %copy-start.4 = (s32[2]{0:T(128)S(1)}, s32[2]{0:T(128)}, u32[]{:S(2)}) copy-start(s32[2]{0:T(128)} %param.9) | copy-start | bytes 28
  16.6 288.4 %all-reduce.2.cloned.1.call-start = ((), (), s32[]{:S(2)}) async-start(), calls=%async_computation.4 | async-start | bytes 6291456 | tf_op jit(solution)/shard_map/psum | solution.py:83
  463.2 2.0 copy-start.2
  626.5 9.7 %copy-start.1 = (bf16[6,128,2048]{2,1,0:T(8,128)(2,1)S(1)}, bf16[6,128,2048]{2,1,0:T(8,128)(2,1)}, u32[]{:S(2)}) copy-start(bf16[6,128,2048]{2,1,0:T(8,128)(2,1)} %param.5) | copy-start | bytes 9437188
Sparse Core Ops, SparseCore 0:
  16.7 214.6 reduce-scatter.1
  234.7 70.3 all-reduce.1
